TPU v7x, 32 devices: a whole 2x2x4 slice. The times are simulated.
32 devices in a mesh: dz: 4 (over z), dy: 2 (over y), dx: 4 (over x, core).
Axes of the slice: x: 2, y: 2, z: 4, core: 2. Of those that a mesh axis runs over, the one named last changes fastest.
Arguments:
- g_emb: float32 [32, 512, 512], P(('dz', 'dy', 'dx'))
- g_attn: float32 [32, 1, 4, 512, 512], P(('dz', 'dy', 'dx'))
- g_in: float32 [32, 1, 512, 2048], P(('dz', 'dy', 'dx'))
- g_out: float32 [32, 1, 2048, 512], P(('dz', 'dy', 'dx'))
- g_vecd: float32 [32, 1, 9, 512], P(('dz', 'dy', 'dx'))
- g_vecf: float32 [32, 1, 2048], P(('dz', 'dy', 'dx'))
- opt_m: float32 [3416064], P(('dz', 'dy', 'dx'))
- opt_v: float32 [3416064], P(('dz', 'dy', 'dx'))
- master: float32 [3416064], P(('dz', 'dy', 'dx'))
- tok_ids: int32 [524288], P(('dz', 'dy', 'dx'))
- act_in: bfloat16 [524288, 512], P(('dz', 'dy', 'dx'))
Outputs:
- output 1: float32 [3416064], P(('dz', 'dy', 'dx'))
- output 2: float32 [3416064], P(('dz', 'dy', 'dx'))
- output 3: float32 [3416064], P(('dz', 'dy', 'dx'))
- output 4: bfloat16 [512, 512], replicated
- output 5: bfloat16 [1, 4, 512, 512], replicated
- output 6: bfloat16 [1, 512, 2048], replicated
- output 7: bfloat16 [1, 2048, 512], replicated
- output 8: bfloat16 [1, 9, 512], replicated
- output 9: bfloat16 [1, 2048], replicated
- output 10: bfloat16 [524288, 512], P(('dz', 'dy', 'dx'))
All inputs are finite; a program needn't handle non-finite values.
Results may differ from a plain program's by a relative error of at most 0.001.
Values are sent between devices in bfloat16 or wider.
A program may use at most 1 GiB of HBM per device.

v0:
```python
import math
import jax
import jax.numpy as jnp
from jax import lax
from jax.sharding import PartitionSpec as P

LEARN_RATE = 0.002
BETA_ONE = 0.9
BETA_TWO = 0.95
ADAM_EPS = 1e-8
ADAM_STEP = 2
AXES = ("dz", "dy", "dx")
GRAD_RANKS = (3, 5, 4, 4, 4, 3)


def adam_update(grad_vals, opt_m, opt_v, master):
    m_new = BETA_ONE * opt_m + (1.0 - BETA_ONE) * grad_vals
    v_new = BETA_TWO * opt_v + (1.0 - BETA_TWO) * grad_vals * grad_vals
    m_hat = m_new / (1.0 - BETA_ONE ** ADAM_STEP)
    v_hat = v_new / (1.0 - BETA_TWO ** ADAM_STEP)
    w_new = master - LEARN_RATE * m_hat / (jnp.sqrt(v_hat) + ADAM_EPS)
    return m_new, v_new, w_new


def split_flat(flat_vals, shapes):
    pieces = []
    offset = 0
    for tensor_shape in shapes:
        elem_count = math.prod(tensor_shape)
        pieces.append(flat_vals[offset:offset + elem_count].reshape(tensor_shape))
        offset = offset + elem_count
    return pieces


def ffn_block(wb_emb, w_in, b_in, w_out, b_out, tok_ids, act_in):
    emb_rows = jnp.take(wb_emb, tok_ids, axis=0).astype(jnp.float32)
    hidden = (emb_rows * math.sqrt(wb_emb.shape[1]) + act_in.astype(jnp.float32)).astype(jnp.bfloat16)
    pre_act = jnp.dot(hidden, w_in, preferred_element_type=jnp.float32) + b_in.astype(jnp.float32)
    inner_act = jax.nn.gelu(pre_act, approximate=True).astype(jnp.bfloat16)
    return (jnp.dot(inner_act, w_out, preferred_element_type=jnp.float32) + b_out.astype(jnp.float32)).astype(jnp.bfloat16)


def solution(mesh):
    devices = math.prod([mesh.shape[axis_name] for axis_name in AXES])

    def device_step(g_emb, g_attn, g_in, g_out, g_vecd, g_vecf, opt_m, opt_v, master, tok_ids, act_in):
        grad_list = [g_emb, g_attn, g_in, g_out, g_vecd, g_vecf]
        shapes = [grad_arr.shape[1:] for grad_arr in grad_list]
        param_count = sum(math.prod(tensor_shape) for tensor_shape in shapes)
        shard_len = opt_m.shape[0]
        local_flat = jnp.concatenate([grad_arr.reshape(-1) for grad_arr in grad_list])
        local_flat = jnp.pad(local_flat, (0, shard_len * devices - param_count))
        grad_shard = lax.psum_scatter(local_flat, AXES, scatter_dimension=0, tiled=True) / devices
        m_new, v_new, w_new = adam_update(grad_shard, opt_m, opt_v, master)
        full_half = lax.all_gather(w_new.astype(jnp.bfloat16), AXES, axis=0, tiled=True)
        wb_emb, wb_attn, wb_in, wb_out, wb_vecd, wb_vecf = split_flat(full_half, shapes)
        y_out = ffn_block(wb_emb, wb_in[0], wb_vecf[0], wb_out[0], wb_vecd[0, 8], tok_ids, act_in)
        return (m_new, v_new, w_new, wb_emb, wb_attn, wb_in, wb_out, wb_vecd, wb_vecf, y_out)

    grad_specs = tuple(P(AXES, *([None] * (grad_rank - 1))) for grad_rank in GRAD_RANKS)
    in_specs = grad_specs + (P(AXES), P(AXES), P(AXES), P(AXES), P(AXES, None))
    out_specs = (P(AXES), P(AXES), P(AXES), P(), P(), P(), P(), P(), P(), P(AXES, None))
    return jax.shard_map(device_step, mesh=mesh, in_specs=in_specs, out_specs=out_specs, check_vma=False)
```

profile of v0, /device:TPU:1, one launch (start us, length us, event | category | flops | bytes accessed | tf_op | source)
XLA Modules:
  0.0 742.0 jit_solution(8932476508316797493)
XLA Ops:
  7.2 0.0 all-reduce.4.cloned.1.call-start
  7.2 0.8 reduce
  8.0 1.7 copy.21
  9.7 3.3 copy.22
  13.0 3.1 copy.23
  16.1 1.1 copy.24
  17.2 0.1 constant_dynamic-update-slice_fusion.5
  17.3 0.3 constant_dynamic-update-slice_fusion.4
  17.5 0.3 constant_dynamic-update-slice_fusion.3
  17.8 0.3 constant_dynamic-update-slice_fusion.2
  18.1 5.5 pad.4
  23.7 0.0 all-reduce.4.cloned.1.call-update
  23.7 0.0 all-gather.3.cloned.1.call-start
  23.8 245.7 %all-reduce.4.cloned.1.call-done = f32[3416064]{0:T(1024)} async-done(((f32[3416064]{0:T(1024)}), f32[3416064]{0:T(1024)}) %all-reduce.4.cloned.1.call-update) | async-done | bytes 13664272
  269.5 2.4 fusion.27
  271.9 1.0 reshape.112
  273.0 100.2 %all-gather.3.cloned.1.call-done = bf16[32,1,106752]{2,1,0:T(2,128)(2,1)} async-done(((bf16[1,1,106752]{2,1,0:T(2,128)(2,1)}), bf16[32,1,106752]{2,1,0:T(2,128)(2,1)}) %all-gather.3.cloned.1.call-update) | async-done | bytes 6832144 | tf_op jit(solution)/shard_map/all_gather | solution.py:55
  373.1 140.6 %reduce.1 = bf16[32,106752]{1,0:T(8,128)(2,1)} reduce(bf16[32,1,106752]{2,1,0:T(2,128)(2,1)} %all-gather.3.cloned.1.call-done, bf16[]{:T(256)} %constant.64), dimensions={1}, to_apply=%all-gather.reduce_sub_computation | reduce | bytes 13664258 | tf_op jit(solution)/shard_map/all_gather | solution.py:55
  513.8 13.0 %reshape.113 = bf16[3416064]{0:T(1024)(128)(2,1)} reshape(bf16[32,106752]{1,0:T(8,128)(2,1)} %reduce.1) | data formatting | bytes 13664256
  526.7 0.7 slice_convert_fusion.1
  527.4 5.3 fusion.28
  532.7 4.4 slice.59
  537.1 4.3 reshape.99
  541.4 2.3 slice.58
  543.7 2.3 reshape.98
  546.0 0.6 slice_convert_fusion
  546.6 0.6 reshape.101
  547.2 0.3 slice.52
  547.6 4.5 reshape.97
  552.1 66.4 %gather_fusion = bf16[16384,512]{1,0:T(8,128)(2,1)} fusion(bf16[512,512]{1,0:T(8,128)(2,1)S(1)} %slice.52, s32[16384]{0:T(1024)S(1)} %fusion.18), kind=kCustom, calls=%fused_computation | custom fusion | bytes 33619968 | tf_op jit(solution)/shard_map/jit(_take)/gather | solution.py:36
  618.5 73.0 %fusion.37 = bf16[16384,2048]{1,0:T(8,128)(2,1)} fusion(f32[2048]{0:T(1024)S(1)} %get-tuple-element.14, bf16[512,2048]{1,0:T(8,128)(2,1)} %slice.58, bf16[16384,512]{1,0:T(8,128)(2,1)} %param.21, bf16[16384,512]{1,0:T(8,128)(2,1)} %gather_fusion, pred[16384]{0:T(1024)(128)(4,1)S(1)} %compare_and_fusion), kind=kOutput, calls=%fused_computation.9.clone.clone.clone.clone.1 | convolution fusion | flops 34745614336 | bytes 102785024 | tf_op jit(solution)/shard_map/dot_general | solution.py:38
  691.4 43.7 %add_convert_fusion = bf16[16384,512]{1,0:T(8,128)(2,1)} fusion(bf16[2048,512]{1,0:T(8,128)(2,1)S(1)} %copy-done.2, f32[512]{0:T(512)S(1)} %bitcast.26, bf16[16384,2048]{1,0:T(8,128)(2,1)} %fusion.37), kind=kOutput, calls=%fused_computation.11 | convolution fusion | flops 34376515584 | bytes 85985280 | tf_op jit(solution)/shard_map/dot_general | solution.py:40
  (31 shorter events, 0.2 us)
Async XLA Ops:
  7.2 262.3 %all-reduce.4.cloned.1.call-start = ((), (), s32[]{:S(2)}) async-start(), calls=%async_computation.1 | async-start | bytes 27328512
  8.0 8.1 %copy-start.1 = (f32[1,1,2048,512]{3,2,1,0:T(8,128)S(1)}, f32[1,1,2048,512]{3,2,1,0:T(8,128)}, u32[]{:S(2)}) copy-start(f32[1,1,2048,512]{3,2,1,0:T(8,128)} %param.14) | copy-start | bytes 12582916
  17.2 0.9 copy-start.8
  23.7 245.8 %copy-start.3 = (f32[106752]{0:T(1024)S(1)}, f32[106752]{0:T(1024)}, u32[]{:S(2)}) copy-start(f32[106752]{0:T(1024)} %param.19) | copy-start | bytes 1281028
  23.7 245.8 %copy-start.4 = (f32[106752]{0:T(1024)S(1)}, f32[106752]{0:T(1024)}, u32[]{:S(2)}) copy-start(f32[106752]{0:T(1024)} %param.18) | copy-start | bytes 1281028
  23.7 245.8 %copy-start.5 = (f32[106752]{0:T(1024)S(1)}, f32[106752]{0:T(1024)}, u32[]{:S(2)}) copy-start(f32[106752]{0:T(1024)} %param.17) | copy-start | bytes 1281028
  23.7 249.2 %copy-start.6 = (s32[16384]{0:T(1024)S(1)}, s32[16384]{0:T(1024)}, u32[]{:S(2)}) copy-start(s32[16384]{0:T(1024)} %param.20) | copy-start | bytes 196612
  23.7 349.4 %all-gather.3.cloned.1.call-start = ((), (), s32[]{:S(2)}) async-start(), calls=%async_computation | async-start | bytes 14091264 | tf_op jit(solution)/shard_map/all_gather | solution.py:55
  527.4 18.6 %slice-start = ((bf16[3416064]{0:T(1024)(128)(2,1)}), bf16[4608]{0:T(1024)(128)(2,1)S(1)}, s32[]{:S(2)}) async-start(bf16[3416064]{0:T(1024)(128)(2,1)} %reshape.113), calls=%async_computation.2 | async-start | bytes 20480 | tf_op jit(solution)/shard_map/slice | solution.py:30
  527.4 19.8 %slice-start.1 = ((bf16[3416064]{0:T(1024)(128)(2,1)}), bf16[262144]{0:T(1024)(128)(2,1)S(1)}, s32[]{:S(2)}) async-start(bf16[3416064]{0:T(1024)(128)(2,1)} %reshape.113), calls=%async_computation.3 | async-start | bytes 1048576 | tf_op jit(solution)/shard_map/slice | solution.py:30
  546.0 0.6 copy-start.7
  547.5 70.9 %copy-start = (bf16[512,512]{1,0:T(8,128)(2,1)}, bf16[512,512]{1,0:T(8,128)(2,1)S(1)}, u32[]{:S(2)}) copy-start(bf16[512,512]{1,0:T(8,128)(2,1)S(1)} %slice.52) | copy-start | bytes 1572868
  618.4 73.0 %copy-start.2 = (bf16[2048,512]{1,0:T(8,128)(2,1)S(1)}, bf16[2048,512]{1,0:T(8,128)(2,1)}, u32[]{:S(2)}) copy-start(bf16[2048,512]{1,0:T(8,128)(2,1)} %slice.59) | copy-start | bytes 6291460
  618.5 73.0 %copy-start.9 = (f32[1,1,512]{2,1,0:T(1,128)S(1)}, f32[1,1,512]{2,1,0:T(1,128)}, u32[]{:S(2)}) copy-start(f32[1,1,512]{2,1,0:T(1,128)} %slice_convert_fusion) | copy-start | bytes 6148
Sparse Core Ops, SparseCore 0:
  23.8 245.5 all-reduce.3
  273.0 100.0 all-gather.2
where the time goes:
time: 743 us; the launch traced here: 742 us
  waiting for transfers between devices  346 us (47%)
  other arithmetic  145 us (20%)
  local copies, waits for them, and re-layouts  120 us (16%)
  matrix products  117 us (16%)
  between operations  14.2 us (2%)
    unnamed x3, waiting for transfers between devices  246 us
    all_gather x1, other arithmetic, device_step(): lax.all_gather(w_new.astype(jnp.bfloat16), AXES, axis=0, tiled=True)  141 us
    all_gather x1, waiting for transfers between devices, device_step(): lax.all_gather(w_new.astype(jnp.bfloat16), AXES, axis=0, tiled=True)  100 us
    dot_general x1, matrix products, ffn_block(): jnp.dot(hidden, w_in, preferred_element_type=jnp.float32)  73 us
    gather x1, local copies, waits for them, and re-layouts, ffn_block(): emb_rows = jnp.take(wb_emb, tok_ids, axis=0).astype(jnp.float32)  66.4 us
    dot_general x1, matrix products, ffn_block(): jnp.dot(inner_act, w_out, preferred_element_type=jnp.float32)  43.7 us
    unnamed x31, local copies, waits for them, and re-layouts  24 us
  transfers between devices with their start and end apart: 2, of which 2 were waited for; matrix products, arithmetic and copies ran while one was open for 0% of the time, Pallas kernels for 0%

commit v1 on v0

v1 whole, which is shorter than its diff:
```python
import functools
import math

import jax
import jax.numpy as jnp
from jax import lax
from jax.experimental import pallas as pl
from jax.experimental.pallas import tpu as pltpu
from jax.sharding import PartitionSpec as P

LEARN_RATE = 0.002
BETA_ONE = 0.9
BETA_TWO = 0.95
ADAM_EPS = 1e-8
ADAM_STEP = 2
AXES = ("dz", "dy", "dx")
GRAD_RANKS = (3, 5, 4, 4, 4, 3)
MESH = pl.DeviceIdType.MESH
F32, BF16 = jnp.float32, jnp.bfloat16

D, FF, VOCAB = 512, 2048, 512
ROWS = 26688
SHARD = 834
WIN = 840
WROWS = 848
TENSORS = ((0, 512, 512), (2048, 2048, 512), (10240, 512, 2048), (18432, 2048, 512))
VEC_ROW = 26624
COLORS = (
    ((0, 1, 2, 3), (0, 208), (0, 208)),
    ((1, 2, 3, 0), (208, 208), (208, 208)),
    ((2, 3, 0, 1), (416, 208), (416, 208)),
    ((3, 0, 1, 2), (624, 216), (624, 224)),
)
NC = len(COLORS)


def adam_update(grad_vals, opt_m, opt_v, master):
    m_new = BETA_ONE * opt_m + (1.0 - BETA_ONE) * grad_vals
    v_new = BETA_TWO * opt_v + (1.0 - BETA_TWO) * grad_vals * grad_vals
    m_hat = m_new / (1.0 - BETA_ONE ** ADAM_STEP)
    v_hat = v_new / (1.0 - BETA_TWO ** ADAM_STEP)
    w_new = master - LEARN_RATE * m_hat / (jnp.sqrt(v_hat) + ADAM_EPS)
    return m_new, v_new, w_new


def window_start(s):
    return (s // 4) * 3336 + (s % 4) * 832


def comm_kernel(ge, ga, gi, go, gv, m_in, v_in, w_in, m_out, v_out, w_out, wg_out,
                ne, na, ni, no, flat, acc, r0, r1, r2, r3, r4, ms, vs, ws, wg,
                ld_sem, mvw_sem, s0_s, s0_r, rs_s, rs_r, ag_s, ag_r, pc_s, pc_r, out_sem):
    z, y, xc = lax.axis_index("dz"), lax.axis_index("dy"), lax.axis_index("dx")
    x, c = xc // 2, xc % 2
    b1, b0 = z // 2, z % 2
    g0 = (b0 + b1) % 2
    bits = (b1, g0, y, x)
    peer = (z, y, 2 * x + 1 - c)
    partner = ((3 - z, y, xc), (2 * b1 + 1 - b0, y, xc), (z, 1 - y, xc), (z, y, 2 * (1 - x) + c))

    native = (ne, na, ni, no)
    loads = []
    n_load = 0
    for t, (src, dst, (base, rows, cols)) in enumerate(zip((ge, ga, gi, go), native, TENSORS)):
        chunk = 131072 // cols
        for r in range(0, rows, chunk):
            cp = pltpu.make_async_copy(src.at[pl.ds(r, chunk)], dst.at[pl.ds(r, chunk)], ld_sem.at[n_load])
            cp.start()
            loads.append((cp, t, r, chunk, base + (r + chunk) * cols // 128))
            n_load += 1
    vec_cp = pltpu.make_async_copy(gv, flat.at[pl.ds(VEC_ROW, 64)], ld_sem.at[n_load])
    vec_cp.start()
    mvw = []
    for i, (a, b) in enumerate(((m_in, ms), (v_in, vs), (w_in, ws))):
        cp = pltpu.make_async_copy(a, b, mvw_sem.at[i])
        cp.start()
        mvw.append(cp)

    barrier = pltpu.get_barrier_semaphore()
    for dev in (peer,) + partner:
        pl.semaphore_signal(barrier, inc=1, device_id=dev, device_id_type=MESH)
    pl.semaphore_wait(barrier, 5)

    s0 = []

    def send0(i):
        start = pl.multiple_of(window_start(2 * i + 1 - c), 8)
        cp = pltpu.make_async_remote_copy(flat.at[pl.ds(start, WIN)], r0.at[i], s0_s.at[i], s0_r.at[i],
                                          device_id=peer, device_id_type=MESH)
        cp.start()
        s0.append(cp)

    vec_cp.wait()
    for cp, t, r, chunk, end in loads:
        cp.wait()
        base, _, cols = TENSORS[t]
        lanes = cols // 128

        def group(g, carry, t=t, r=r, base=base, lanes=lanes):
            row = pl.multiple_of(r + g * 8, 8)
            out = base + row * lanes
            for j in range(lanes):
                flat[pl.ds(out + j, 8, stride=lanes), :] = native[t][pl.ds(row, 8), j * 128:(j + 1) * 128]
            return carry

        lax.fori_loop(0, chunk // 8, group, 0, unroll=4 if lanes == 4 else 1)
        if end == VEC_ROW:
            end = ROWS
        while len(s0) < 16 and window_start(2 * len(s0) + 1) + WIN <= end:
            send0(len(s0))

    def slot(i):
        zz = i // 4
        return (zz // 2, (zz % 2 + zz // 2) % 2, (i // 2) % 2, i % 2)

    for i in range(16):
        s0[i].wait_recv()
        start = pl.multiple_of(window_start(2 * i + c), 8)
        acc[slot(i)] = flat[pl.ds(start, WIN), :] + r0[i]

    recv = (r1, r2, r3, r4)
    full = pl.ds(0, 2)

    def rs_copy(k, t):
        order, (row, n), _ = COLORS[k]
        idx = [full] * 4
        for d in order[:t]:
            idx[d] = bits[d]
        idx[order[t]] = 1 - bits[order[t]]
        dst = recv[t].at[(full,) * (3 - t) + (pl.ds(row, n),)]
        return pltpu.make_async_remote_copy(acc.at[tuple(idx) + (pl.ds(row, n),)], dst, rs_s.at[k, t], rs_r.at[k, t],
                                            device_id=partner[order[t]], device_id_type=MESH)

    def rs_add(k, t):
        order, (row, n), _ = COLORS[k]
        idx = [None] * 4
        for d in order[:t + 1]:
            idx[d] = bits[d]
        rest = [d for d in range(4) if idx[d] is None]
        for combo in range(2 ** len(rest)):
            sub = tuple((combo >> (len(rest) - 1 - j)) & 1 for j in range(len(rest)))
            for j, d in enumerate(rest):
                idx[d] = sub[j]
            acc[tuple(idx) + (pl.ds(row, n),)] += recv[t][sub + (pl.ds(row, n),)]

    rs = {}
    for k in range(NC):
        rs[k, 0] = rs_copy(k, 0)
        rs[k, 0].start()
    for t in range(4):
        for k in range(NC):
            rs[k, t].wait_recv()
            rs_add(k, t)
            if t < 3:
                rs[k, t + 1] = rs_copy(k, t + 1)
                rs[k, t + 1].start()

    for cp in mvw:
        cp.wait()
    q = 2 * x + c
    for case in range(4):
        @pl.when(q == case)
        def _():
            grad = acc[bits + (pl.ds(2 * case, SHARD),)] / 32.0
            m_new, v_new, w_new = adam_update(grad, ms[...], vs[...], ws[...])
            ms[...] = m_new
            vs[...] = v_new
            ws[...] = w_new
            wg[(c,) + bits + (pl.ds(SHARD - 2, 16),)] = jnp.zeros((16, 128), BF16)
            wg[(c,) + bits + (pl.ds(0, SHARD),)] = w_new.astype(BF16)
    outs = []
    for i, (a, b) in enumerate(((ms, m_out), (vs, v_out), (ws, w_out))):
        cp = pltpu.make_async_copy(a, b, out_sem.at[i])
        cp.start()
        outs.append(cp)

    def ag_idx(k, t, mine):
        order = COLORS[k][0]
        idx = [full] * 4
        for d in order[:t]:
            idx[d] = bits[d]
        if t < 4:
            idx[order[t]] = bits[order[t]] if mine else 1 - bits[order[t]]
        return (c,) + tuple(idx) + (pl.ds(*COLORS[k][2]),)

    def ag_copy(k, t):
        ref = wg.at[ag_idx(k, t, True)]
        return pltpu.make_async_remote_copy(ref, ref, ag_s.at[k, t], ag_r.at[k, t],
                                            device_id=partner[COLORS[k][0][t]], device_id_type=MESH)

    def pc_copy(k, t):
        ref = wg.at[ag_idx(k, t, False) if t < 4 else (c,) + bits + (pl.ds(*COLORS[k][2]),)]
        return pltpu.make_async_remote_copy(ref, ref, pc_s.at[k, t], pc_r.at[k, t],
                                            device_id=peer, device_id_type=MESH)

    ag, pc = {}, {}
    for k in range(NC):
        ag[k, 3] = ag_copy(k, 3)
        ag[k, 3].start()
    for k in range(NC):
        pc[k, 4] = pc_copy(k, 4)
        pc[k, 4].start()
    for t in (3, 2, 1, 0):
        for k in range(NC):
            ag[k, t].wait_recv()
            if t > 0:
                ag[k, t - 1] = ag_copy(k, t - 1)
                ag[k, t - 1].start()
            pc[k, t] = pc_copy(k, t)
            pc[k, t].start()
    for t in (4, 3, 2, 1, 0):
        for k in range(NC):
            pc[k, t].wait_recv()
    cp = pltpu.make_async_copy(wg, wg_out, out_sem.at[3])
    cp.start()
    outs.append(cp)
    for cp in s0 + list(rs.values()) + list(ag.values()) + list(pc.values()):
        cp.wait_send()
    for cp in outs:
        cp.wait()


def comm(ge, ga, gi, go, gv, m, v, w):
    any_spec = pl.BlockSpec(memory_space=pl.ANY)
    shard = jax.ShapeDtypeStruct((SHARD, 128), F32)
    dma = pltpu.SemaphoreType.DMA
    return pl.pallas_call(
        comm_kernel,
        out_shape=(shard, shard, shard, jax.ShapeDtypeStruct((2, 2, 2, 2, 2, WROWS, 128), BF16)),
        in_specs=[any_spec] * 8,
        out_specs=(any_spec,) * 4,
        scratch_shapes=[
            pltpu.VMEM((512, 512), F32), pltpu.VMEM((2048, 512), F32),
            pltpu.VMEM((512, 2048), F32), pltpu.VMEM((2048, 512), F32),
            pltpu.VMEM((ROWS, 128), F32),
            pltpu.VMEM((2, 2, 2, 2, WIN, 128), F32),
            pltpu.VMEM((16, WIN, 128), F32),
            pltpu.VMEM((2, 2, 2, WIN, 128), F32), pltpu.VMEM((2, 2, WIN, 128), F32),
            pltpu.VMEM((2, WIN, 128), F32), pltpu.VMEM((WIN, 128), F32),
            pltpu.VMEM((SHARD, 128), F32), pltpu.VMEM((SHARD, 128), F32), pltpu.VMEM((SHARD, 128), F32),
            pltpu.VMEM((2, 2, 2, 2, 2, WROWS, 128), BF16),
            dma((32,)), dma((3,)), dma((16,)), dma((16,)),
            dma((NC, 4)), dma((NC, 4)), dma((NC, 4)), dma((NC, 4)), dma((NC, 5)), dma((NC, 5)), dma((4,)),
        ],
        compiler_params=pltpu.CompilerParams(collective_id=0, has_side_effects=True, vmem_limit_bytes=66_000_000),
        name="comm",
    )(ge, ga, gi, go, gv, m, v, w)


def unpack_kernel(wg, we, wa, wi, wo, wv, flat):
    for s in range(32):
        i, core = s // 2, s % 2
        zz = i // 4
        idx = (core, zz // 2, (zz % 2 + zz // 2) % 2, (i // 2) % 2, i % 2)
        flat[pl.ds(s * SHARD, SHARD), :] = wg[idx + (pl.ds(0, SHARD),)].astype(F32)
    for dst, (base, rows, cols) in zip((we, wa, wi, wo), TENSORS):
        lanes = cols // 128

        def group(g, carry, dst=dst, base=base, lanes=lanes):
            row = pl.multiple_of(g * 16, 16)
            for j in range(lanes):
                dst[pl.ds(row, 16), j * 128:(j + 1) * 128] = flat[
                    pl.ds(base + row * lanes + j, 16, stride=lanes), :].astype(BF16)
            return carry

        lax.fori_loop(0, rows // 16, group, 0, unroll=4 if lanes == 4 else 1)
    wv[...] = flat[pl.ds(VEC_ROW, 64), :].astype(BF16)


def unpack(wg):
    vm = pl.BlockSpec(memory_space=pltpu.VMEM)
    shapes = [(512, 512), (2048, 512), (512, 2048), (2048, 512), (64, 128)]
    return pl.pallas_call(
        unpack_kernel,
        out_shape=tuple(jax.ShapeDtypeStruct(s, BF16) for s in shapes),
        in_specs=[vm],
        out_specs=(vm,) * 5,
        scratch_shapes=[pltpu.VMEM((ROWS, 128), F32)],
        compiler_params=pltpu.CompilerParams(vmem_limit_bytes=60_000_000),
        name="unpack",
    )(wg)


TM = 512


def gelu_tanh(v):
    return v * (0.5 * (1.0 + jnp.tanh(math.sqrt(2.0 / math.pi) * (v + 0.044715 * (v * v * v)))))


def ffn_kernel(tok, act, we, wi, bi, wo, bo, out):
    lane = lax.broadcasted_iota(jnp.int32, (TM, 128), 1)
    col = jnp.transpose(jnp.broadcast_to(tok[0], (128, TM)), (1, 0))
    hot = jnp.concatenate([(col == lane + 128 * j).astype(F32).astype(BF16) for j in range(VOCAB // 128)], axis=1)
    rows = jnp.dot(hot, we[...], preferred_element_type=F32)
    hidden = (rows * math.sqrt(D) + act[...].astype(F32)).astype(BF16)
    step = 512
    total = None
    pre = jnp.dot(hidden, wi[:, 0:step], preferred_element_type=F32)
    for f in range(0, FF, step):
        nxt = None
        if f + step < FF:
            nxt = jnp.dot(hidden, wi[:, f + step:f + 2 * step], preferred_element_type=F32)
        inner = gelu_tanh(pre + bi[:, f:f + step].astype(F32)).astype(BF16)
        part = jnp.dot(inner, wo[f:f + step, :], preferred_element_type=F32)
        total = part if total is None else total + part
        pre = nxt
    out[...] = (total + bo[...].astype(F32)).astype(BF16)


def ffn(tok, act, we, wi, bi, wo, bo):
    tokens = act.shape[0]
    const = lambda i: (0, 0)
    return pl.pallas_call(
        ffn_kernel,
        grid=(tokens // TM,),
        out_shape=jax.ShapeDtypeStruct((tokens, D), BF16),
        in_specs=[
            pl.BlockSpec((1, 1, TM), lambda i: (i, 0, 0)),
            pl.BlockSpec((TM, D), lambda i: (i, 0)),
            pl.BlockSpec((VOCAB, D), const),
            pl.BlockSpec((D, FF), const),
            pl.BlockSpec((1, FF), const),
            pl.BlockSpec((FF, D), const),
            pl.BlockSpec((1, D), const),
        ],
        out_specs=pl.BlockSpec((TM, D), lambda i: (i, 0)),
        compiler_params=pltpu.CompilerParams(vmem_limit_bytes=60_000_000),
        name="ffn",
    )(tok.reshape(tokens // TM, 1, TM), act, we, wi, bi, wo, bo)


def solution(mesh):
    def device_step(g_emb, g_attn, g_in, g_out, g_vecd, g_vecf, opt_m, opt_v, master, tok_ids, act_in):
        gv = jnp.concatenate([g_vecd.reshape(36, 128), g_vecf.reshape(16, 128), jnp.zeros((12, 128), F32)], axis=0)
        m_new, v_new, w_new, wg = comm(
            g_emb.reshape(512, 512), g_attn.reshape(2048, 512), g_in.reshape(512, 2048), g_out.reshape(2048, 512), gv,
            opt_m.reshape(SHARD, 128), opt_v.reshape(SHARD, 128), master.reshape(SHARD, 128))
        we, wa, wi, wo, wv = unpack(wg)
        vecd = wv[:36].reshape(1, 9, 512)
        vecf = wv[36:52].reshape(1, 2048)
        y_out = ffn(tok_ids, act_in, we, wi, vecf, wo, vecd[0, 8:9])
        return (m_new.reshape(-1), v_new.reshape(-1), w_new.reshape(-1), we, wa.reshape(1, 4, 512, 512),
                wi.reshape(1, 512, 2048), wo.reshape(1, 2048, 512), vecd, vecf, y_out)

    grad_specs = tuple(P(AXES, *([None] * (grad_rank - 1))) for grad_rank in GRAD_RANKS)
    in_specs = grad_specs + (P(AXES), P(AXES), P(AXES), P(AXES), P(AXES, None))
    out_specs = (P(AXES), P(AXES), P(AXES), P(), P(), P(), P(), P(), P(), P(AXES, None))
    return jax.shard_map(device_step, mesh=mesh, in_specs=in_specs, out_specs=out_specs, check_vma=False)
```

time: 743 us -> 266 us (0.36)
  waiting for transfers between devices: 346 us -> 0 us
  Pallas kernels: 0 us -> 256 us
  other arithmetic: 145 us -> 2.16 us
  matrix products: 117 us -> 0 us
  local copies, waits for them, and re-layouts: 120 us -> 5.06 us
  between operations: 14.2 us -> 0.69 us
    pallas_call x0 -> x3, Pallas kernels: none -> 256 us  [the longest x1 140 us: comm(): pl.pallas_call(comm_kernel, out_shape=(shard, shard, shard, jax.ShapeDtyp...]
    unnamed x3 -> x0, waiting for transfers between devices: 246 us -> none
    all_gather x1 -> x0, other arithmetic: 141 us -> none  [device_step(): lax.all_gather(w_new.astype(jnp.bfloat16), AXES, axis=0, tiled=True)]
    dot_general x2 -> x0, matrix products: 117 us -> none  [the longest x1 73 us: ffn_block(): jnp.dot(hidden, w_in, preferred_element_type=jnp.float32)]
    all_gather x1 -> x0, waiting for transfers between devices: 100 us -> none  [device_step(): lax.all_gather(w_new.astype(jnp.bfloat16), AXES, axis=0, tiled=True)]
    gather x1 -> x0, local copies, waits for them, and re-layouts: 66.4 us -> none  [ffn_block(): emb_rows = jnp.take(wb_emb, tok_ids, axis=0).astype(jnp.float32)]
    unnamed x31 -> x13, local copies, waits for them, and re-layouts: 24 us -> 3.68 us
    reshape x6 -> x2, local copies, waits for them, and re-layouts: 11.8 us -> 0.02 us  [the longest x1 0.02 us: device_step(): vecd = wv[:36].reshape(1, 9, 512)]
  transfers between devices with their start and end apart: 2 -> 0, of which waited for: 2 -> 0; matrix products, arithmetic and copies ran while one was open for 0% -> 0% of each run, Pallas kernels for 0% -> 0%
where the time goes in v1:
time: 266 us; the launch traced here: 264 us
  Pallas kernels  256 us (96%)
  local copies, waits for them, and re-layouts  5.06 us (2%)
    pallas_call x1, Pallas kernels, comm(): pl.pallas_call(comm_kernel, out_shape=(shard, shard, shard, jax.ShapeDtyp...  140 us
    pallas_call x1, Pallas kernels, ffn(): pl.pallas_call(ffn_kernel, grid=(tokens // TM,), out_shape=jax.ShapeDtype...  107 us
    pallas_call x1, Pallas kernels, unpack(): pl.pallas_call(unpack_kernel, out_shape=tuple((jax.ShapeDtypeStruct(s, BF...  9.46 us

profile of v1, /device:TPU:1, one launch (start us, length us, event | category | flops | bytes accessed | tf_op | source)
XLA Modules:
  0.0 264.1 jit_solution(6925889207778311664)
XLA Ops:
  0.7 0.1 pad.2.clone
  0.7 0.8 reduce
  1.5 1.4 maximum_maximum_fusion.gv
  2.9 139.6 %comm.1 = (f32[834,128]{1,0:T(8,128)}, f32[834,128]{1,0:T(8,128)}, f32[834,128]{1,0:T(8,128)}, bf16[2,2,2,2,2,848,128]{6,5,4,3,2,1,0:T(8,128)(2,1)}) custom-call(f32[512,512]{1,0:T(8,128)} %bitcast.28, f32[2048,512]{1,0:T(8,128)} %bitcast.23, f32[512,2048]{1,0:T(8,128)} %bitcast.24, f32[2048,512]{1,0:T(8,128)} %bitcast.25, ...), custom_call_target="tpu_custom_call" | custom-call | tf_op jit(solution)/shard_map/comm/pallas_call | solution.py:227
  142.5 9.5 %unpack.1 = (bf16[512,512]{1,0:T(8,128)(2,1)}, bf16[2048,512]{1,0:T(8,128)(2,1)}, bf16[512,2048]{1,0:T(8,128)(2,1)}, bf16[2048,512]{1,0:T(8,128)(2,1)}, bf16[64,128]{1,0:T(8,128)(2,1)}) custom-call(bf16[2,2,2,2,2,848,128]{6,5,4,3,2,1,0:T(8,128)(2,1)} %get-tuple-element.22.wg), custom_call_target="tpu_custom_call" | custom-call | tf_op jit(solution)/shard_map/unpack/pallas_call | solution.py:273
  151.9 0.7 slice_bitcast_fusion
  152.6 0.7 slice.9
  153.3 0.6 copy.23
  154.0 0.0 copy-start.3
  154.0 0.6 slice_bitcast_fusion.1.bo
  154.6 0.0 copy-start.2
  154.6 0.0 copy-start.1
  154.6 0.0 copy-start
  154.6 107.1 %ffn.1 = bf16[16384,512]{1,0:T(8,128)(2,1)} custom-call(s32[32,1,512]{2,1,0:T(1,128)} %bitcast.35, bf16[16384,512]{1,0:T(8,128)(2,1)} %act.1, bf16[512,512]{1,0:T(8,128)(2,1)} %get-tuple-element.41.we, bf16[512,2048]{1,0:T(8,128)(2,1)} %get-tuple-element.25.wi, bf16[1,2048]{1,0:T(2,128)(2,1)} %bitcast.36, bf16[2048,512]{1,0:T(8,128)(2,1)} %get-tuple-element.26.wo, ...), custom_call_target="tpu_custom_call" | custom-call | tf_op jit(solution)/shard_map/ffn/pallas_call | solution.py:314
  261.7 0.0 copy-done.3
  261.7 0.0 copy-done.2
  261.7 0.8 copy.27
  262.5 0.0 copy-done.1
  262.5 0.8 copy.28
  263.3 0.0 copy-done
  263.3 0.8 copy.29
  (3 shorter events, 0.0 us)
Async XLA Ops:
  154.0 107.7 %copy-start.3 = (bf16[1,9,512]{2,1,0:T(8,128)(2,1)}, bf16[1,9,512]{2,1,0:T(8,128)(2,1)S(1)}, u32[]{:S(2)}) copy-start(bf16[1,9,512]{2,1,0:T(8,128)(2,1)S(1)} %reshape.89) | copy-start | bytes 27652
  154.6 107.1 %copy-start.2 = (f32[834,128]{1,0:T(8,128)S(1)}, f32[834,128]{1,0:T(8,128)}, u32[]{:S(2)}) copy-start(f32[834,128]{1,0:T(8,128)} %get-tuple-element.19) | copy-start | bytes 1281028
  154.6 107.9 %copy-start.1 = (f32[834,128]{1,0:T(8,128)S(1)}, f32[834,128]{1,0:T(8,128)}, u32[]{:S(2)}) copy-start(f32[834,128]{1,0:T(8,128)} %get-tuple-element.20) | copy-start | bytes 1281028
  154.6 108.7 %copy-start = (f32[834,128]{1,0:T(8,128)S(1)}, f32[834,128]{1,0:T(8,128)}, u32[]{:S(2)}) copy-start(f32[834,128]{1,0:T(8,128)} %get-tuple-element.21) | copy-start | bytes 1281028

commit v2 on v1

--- a/solution.py
+++ b/solution.py
@@ -26,10 +26,12 @@
 TENSORS = ((0, 512, 512), (2048, 2048, 512), (10240, 512, 2048), (18432, 2048, 512))
 VEC_ROW = 26624
 COLORS = (
-    ((0, 1, 2, 3), (0, 208), (0, 208)),
-    ((1, 2, 3, 0), (208, 208), (208, 208)),
-    ((2, 3, 0, 1), (416, 208), (416, 208)),
-    ((3, 0, 1, 2), (624, 216), (624, 224)),
+    ((3, 2, 1, 0), (0, 136), (0, 144)),
+    ((3, 2, 0, 1), (136, 144), (144, 144)),
+    ((2, 3, 1, 0), (280, 136), (288, 144)),
+    ((2, 3, 0, 1), (416, 144), (432, 144)),
+    ((1, 0, 3, 2), (560, 136), (576, 144)),
+    ((0, 1, 2, 3), (696, 144), (720, 128)),
 )
 NC = len(COLORS)
 
@@ -281,11 +283,13 @@
     )(wg)
 
 
-TM = 512
+TM = 1024
 
 
 def gelu_tanh(v):
-    return v * (0.5 * (1.0 + jnp.tanh(math.sqrt(2.0 / math.pi) * (v + 0.044715 * (v * v * v)))))
+    c = math.sqrt(2.0 / math.pi)
+    half = 0.5 * v
+    return half + half * jnp.tanh(v * (c + (c * 0.044715) * (v * v)))
 
 
 def ffn_kernel(tok, act, we, wi, bi, wo, bo, out):
@@ -295,16 +299,16 @@
     rows = jnp.dot(hot, we[...], preferred_element_type=F32)
     hidden = (rows * math.sqrt(D) + act[...].astype(F32)).astype(BF16)
     step = 512
-    total = None
+    parts = []
     pre = jnp.dot(hidden, wi[:, 0:step], preferred_element_type=F32)
     for f in range(0, FF, step):
         nxt = None
         if f + step < FF:
             nxt = jnp.dot(hidden, wi[:, f + step:f + 2 * step], preferred_element_type=F32)
-        inner = gelu_tanh(pre + bi[:, f:f + step].astype(F32)).astype(BF16)
-        part = jnp.dot(inner, wo[f:f + step, :], preferred_element_type=F32)
-        total = part if total is None else total + part
+        parts.append(gelu_tanh(pre + bi[:, f:f + step].astype(F32)).astype(BF16))
         pre = nxt
+    inner = jnp.concatenate(parts, axis=1)
+    total = jnp.dot(inner, wo[...], preferred_element_type=F32)
     out[...] = (total + bo[...].astype(F32)).astype(BF16)
 
 

time: 266 us -> 227 us (0.85)
  Pallas kernels: 256 us -> 219 us
    pallas_call x1, Pallas kernels: 140 us -> 117 us  [comm(): pl.pallas_call(comm_kernel, out_shape=(shard, shard, shard, jax.ShapeDtyp...]
    pallas_call x1, Pallas kernels: 107 us -> 92.7 us  [ffn(): pl.pallas_call(ffn_kernel, grid=(tokens // TM,), out_shape=jax.ShapeDtype...]
where the time goes in v2:
time: 227 us
  Pallas kernels  219 us (96%)
  local copies, waits for them, and re-layouts  5.06 us (2%)
    pallas_call x1, Pallas kernels, comm(): pl.pallas_call(comm_kernel, out_shape=(shard, shard, shard, jax.ShapeDtyp...  117 us
    pallas_call x1, Pallas kernels, ffn(): pl.pallas_call(ffn_kernel, grid=(tokens // TM,), out_shape=jax.ShapeDtype...  92.7 us
    pallas_call x1, Pallas kernels, unpack(): pl.pallas_call(unpack_kernel, out_shape=tuple((jax.ShapeDtypeStruct(s, BF...  9.46 us

profile of v2, /device:TPU:1, one launch (start us, length us, event | category | flops | bytes accessed | tf_op | source)
XLA Modules:
  0.0 226.8 jit_solution(11016111024528629834)
XLA Ops:
  0.7 0.1 pad.2.clone
  0.7 0.8 reduce
  1.5 1.4 maximum_maximum_fusion.gv
  2.9 116.6 %comm.1 = (f32[834,128]{1,0:T(8,128)}, f32[834,128]{1,0:T(8,128)}, f32[834,128]{1,0:T(8,128)}, bf16[2,2,2,2,2,848,128]{6,5,4,3,2,1,0:T(8,128)(2,1)}) custom-call(f32[512,512]{1,0:T(8,128)} %bitcast.28, f32[2048,512]{1,0:T(8,128)} %bitcast.23, f32[512,2048]{1,0:T(8,128)} %bitcast.24, f32[2048,512]{1,0:T(8,128)} %bitcast.25, ...), custom_call_target="tpu_custom_call" | custom-call | tf_op jit(solution)/shard_map/comm/pallas_call | solution.py:229
  119.5 9.5 %unpack.1 = (bf16[512,512]{1,0:T(8,128)(2,1)}, bf16[2048,512]{1,0:T(8,128)(2,1)}, bf16[512,2048]{1,0:T(8,128)(2,1)}, bf16[2048,512]{1,0:T(8,128)(2,1)}, bf16[64,128]{1,0:T(8,128)(2,1)}) custom-call(bf16[2,2,2,2,2,848,128]{6,5,4,3,2,1,0:T(8,128)(2,1)} %get-tuple-element.22.wg), custom_call_target="tpu_custom_call" | custom-call | tf_op jit(solution)/shard_map/unpack/pallas_call | solution.py:275
  129.0 0.7 slice_bitcast_fusion
  129.7 0.7 slice.9
  130.4 0.6 copy.23
  131.0 0.0 copy-start.3
  131.1 0.6 slice_bitcast_fusion.1.bo
  131.6 0.0 copy-start.2
  131.6 0.0 copy-start.1
  131.6 0.0 copy-start
  131.6 92.7 %ffn.1 = bf16[16384,512]{1,0:T(8,128)(2,1)} custom-call(s32[16,1,1024]{2,1,0:T(1,128)} %bitcast.35, bf16[16384,512]{1,0:T(8,128)(2,1)} %act.1, bf16[512,512]{1,0:T(8,128)(2,1)} %get-tuple-element.41.we, bf16[512,2048]{1,0:T(8,128)(2,1)} %get-tuple-element.25.wi, bf16[1,2048]{1,0:T(2,128)(2,1)} %bitcast.36, bf16[2048,512]{1,0:T(8,128)(2,1)} %get-tuple-element.26.wo, ...), custom_call_target="tpu_custom_call" | custom-call | tf_op jit(solution)/shard_map/ffn/pallas_call | solution.py:318
  224.4 0.0 copy-done.3
  224.4 0.0 copy-done.2
  224.4 0.8 copy.27
  225.2 0.0 copy-done.1
  225.2 0.8 copy.28
  226.0 0.0 copy-done
  226.0 0.8 copy.29
  (3 shorter events, 0.0 us)
Async XLA Ops:
  131.0 93.4 %copy-start.3 = (bf16[1,9,512]{2,1,0:T(8,128)(2,1)}, bf16[1,9,512]{2,1,0:T(8,128)(2,1)S(1)}, u32[]{:S(2)}) copy-start(bf16[1,9,512]{2,1,0:T(8,128)(2,1)S(1)} %reshape.89) | copy-start | bytes 27652
  131.6 92.8 %copy-start.2 = (f32[834,128]{1,0:T(8,128)S(1)}, f32[834,128]{1,0:T(8,128)}, u32[]{:S(2)}) copy-start(f32[834,128]{1,0:T(8,128)} %get-tuple-element.19) | copy-start | bytes 1281028
  131.6 93.5 %copy-start.1 = (f32[834,128]{1,0:T(8,128)S(1)}, f32[834,128]{1,0:T(8,128)}, u32[]{:S(2)}) copy-start(f32[834,128]{1,0:T(8,128)} %get-tuple-element.20) | copy-start | bytes 1281028
  131.6 94.3 %copy-start = (f32[834,128]{1,0:T(8,128)S(1)}, f32[834,128]{1,0:T(8,128)}, u32[]{:S(2)}) copy-start(f32[834,128]{1,0:T(8,128)} %get-tuple-element.21) | copy-start | bytes 1281028

commit v3 on v0

v3 whole, which is shorter than its diff:
```python
import functools
import math

import jax
import jax.numpy as jnp
from jax import lax
from jax.experimental import pallas as pl
from jax.experimental.pallas import tpu as pltpu
from jax.sharding import PartitionSpec as P

LEARN_RATE = 0.002
BETA_ONE = 0.9
BETA_TWO = 0.95
ADAM_EPS = 1e-8
ADAM_STEP = 2
AXES = ("dz", "dy", "dx")
GRAD_RANKS = (3, 5, 4, 4, 4, 3)
MESH = pl.DeviceIdType.MESH
F32, BF16 = jnp.float32, jnp.bfloat16

D, FF, VOCAB, LN = 512, 2048, 512, 128
ROWS = 26688
SHARD = 834
WIN = 840
WROWS = 848
TENSORS = ((0, 512, 512), (2048, 2048, 512), (10240, 512, 2048), (18432, 2048, 512))
VEC_ROW = 26624
X, Y, ZA, ZB = 3, 2, 1, 0
BACK = (3, 2, 1, 0)
ORDERS = ((X, Y, ZA, ZB), (X, Y, ZB, ZA), (Y, X, ZA, ZB), (Y, X, ZB, ZA), (ZA, ZB, X, Y), (ZB, ZA, Y, X))
RS_ROWS = (72, 64, 72, 64, 72, 72, 72, 72, 72, 72, 64, 72)
AG_ROWS = (80, 64, 80, 64, 64, 64, 80, 64, 80, 64, 64, 80)
NC = len(RS_ROWS)
COLORS = tuple((ORDERS[k % len(ORDERS)], (sum(RS_ROWS[:k]), RS_ROWS[k]), (sum(AG_ROWS[:k]), AG_ROWS[k]))
               for k in range(NC))
GROUPS = ((0, sum(RS_ROWS[:6])), (sum(RS_ROWS[:6]), sum(RS_ROWS[6:])))
CHUNK, CHUNK_ROWS = 131072, 1024
RING = 6, 4


def window_start(s):
    return (s // 4) * 3336 + (s % 4) * 832


def adam_update(grad_vals, opt_m, opt_v, master):
    m_new = BETA_ONE * opt_m + (1.0 - BETA_ONE) * grad_vals
    v_new = BETA_TWO * opt_v + (1.0 - BETA_TWO) * grad_vals * grad_vals
    m_hat = m_new / (1.0 - BETA_ONE ** ADAM_STEP)
    v_hat = v_new / (1.0 - BETA_TWO ** ADAM_STEP)
    w_new = master - LEARN_RATE * m_hat / (jnp.sqrt(v_hat) + ADAM_EPS)
    return m_new, v_new, w_new


def window_start(s):
    return (s // 4) * 3336 + (s % 4) * 832


def gelu_tanh(v):
    c = math.sqrt(2.0 / math.pi)
    half = 0.5 * v
    return half + half * jnp.tanh(v * (c + (c * 0.044715) * (v * v)))


def spread(wg, flat, shards):
    for s in shards:
        idx = (s % 2,) + slot(s // 2)
        flat[pl.ds(s * SHARD, SHARD), :] = wg[idx + (pl.ds(0, SHARD),)].astype(F32)


def to_native(flat, dst, tensor, unroll):
    base, rows, cols = TENSORS[tensor]
    lanes = cols // LN

    def group(g, carry):
        row = pl.multiple_of(g * 16, 16)
        for j in range(lanes):
            dst[pl.ds(row, 16), j * LN:(j + 1) * LN] = flat[
                pl.ds(base + row * lanes + j, 16, stride=lanes), :].astype(BF16)
        return carry

    lax.fori_loop(0, rows // 16, group, 0, unroll=unroll)


def slot(i):
    z = i // 4
    return (z // 2, (z % 2 + z // 2) % 2, (i // 2) % 2, i % 2)


def comm_kernel(ge, ga, gi, go, gvd, gvf, m_in, v_in, w_in, m_out, v_out, w_out, we_out, wa_out, wi_out, wo_out,
                wvd_out, wvf_out,
                st5, st20, svd, svf, flat, acc, r1, r2, r3, r4, gs, ms, vs, ws, mo, vo, wn, wg, we, wa, wi, wo, wvd, wvf,
                ld_sem, mvw_sem, s0_s, s0_r, rs_s, rs_r, ag_s, ag_r, pc_s, pc_r, out_sem):
    z, y, xc = lax.axis_index("dz"), lax.axis_index("dy"), lax.axis_index("dx")
    x, c = xc // 2, xc % 2
    b1, b0 = z // 2, z % 2
    g0 = (b0 + b1) % 2
    bits = (b1, g0, y, x)
    peer = (z, y, 2 * x + 1 - c)
    partner = ((3 - z, y, xc), (2 * b1 + 1 - b0, y, xc), (z, 1 - y, xc), (z, y, 2 * (1 - x) + c))

    srcs = (ge, ga, gi, go)
    order = [(t, j) for t, (_, rows, cols) in enumerate(TENSORS) for j in range(rows * cols // CHUNK)]
    seq = ([ch for ch in order if ch[0] != 2], [ch for ch in order if ch[0] == 2])
    ring_of = (st5, st20)

    def load(kind, pos):
        t, j = seq[kind][pos]
        rows = CHUNK // TENSORS[t][2]
        at = pos % RING[kind]
        return pltpu.make_async_copy(srcs[t].at[pl.ds(j * rows, rows)], ring_of[kind].at[at],
                                     ld_sem.at[kind * RING[0] + at])

    for kind in range(2):
        for pos in range(RING[kind]):
            load(kind, pos).start()
    vec = [pltpu.make_async_copy(a, b, ld_sem.at[sum(RING) + i]) for i, (a, b) in enumerate(((gvd, svd), (gvf, svf)))]
    mvw = [pltpu.make_async_copy(a, b, mvw_sem.at[i]) for i, (a, b) in enumerate(((m_in, ms), (v_in, vs), (w_in, ws)))]
    for cp in vec + mvw:
        cp.start()

    barrier = pltpu.get_barrier_semaphore()
    for dev in (peer,) + partner:
        pl.semaphore_signal(barrier, inc=1, device_id=dev, device_id_type=MESH)
    pl.semaphore_wait(barrier, 5)

    done = [0, 0]

    def take(ch):
        t, j = ch
        kind = 1 if t == 2 else 0
        pos = done[kind]
        assert seq[kind][pos] == ch
        load(kind, pos).wait()
        base, _, cols = TENSORS[t]
        lanes = cols // LN
        rows = CHUNK // cols
        slot = pos % RING[kind]
        ring = ring_of[kind]

        def group(g, carry):
            row = pl.multiple_of(g * 8, 8)
            out = base + (j * rows + row) * lanes
            for i in range(lanes):
                flat[pl.ds(out + i, 8, stride=lanes), :] = ring[slot, pl.ds(row, 8), i * LN:(i + 1) * LN]
            return carry

        lax.fori_loop(0, rows // 8, group, 0, unroll=4 if lanes == 4 else 1)
        done[kind] += 1
        if pos + RING[kind] < len(seq[kind]):
            load(kind, pos + RING[kind]).start()

    def s0_copy(i, g):
        row, n = GROUPS[g]
        start = pl.multiple_of(window_start(2 * i + 1 - c) + row, 8)
        return pltpu.make_async_remote_copy(flat.at[pl.ds(start, n)], acc.at[slot(i) + (pl.ds(row, n),)],
                                            s0_s.at[g, i], s0_r.at[g, i], device_id=peer, device_id_type=MESH)

    def s0_add(i, g):
        row, n = GROUPS[g]
        s0_copy(i, g).wait_recv()
        start = pl.multiple_of(window_start(2 * i + c) + row, 8)
        acc[slot(i) + (pl.ds(row, n),)] += flat[pl.ds(start, n), :]

    sent = 0
    for ch in order:
        take(ch)
        end = TENSORS[ch[0]][0] + (ch[1] + 1) * CHUNK_ROWS
        if end == VEC_ROW:
            for cp in vec:
                cp.wait()
            for j in range(4):
                flat[pl.ds(VEC_ROW + j, 9, stride=4), :] = svd[:, j * LN:(j + 1) * LN]
            for j in range(16):
                flat[pl.ds(VEC_ROW + 36 + j, 1), :] = svf[:, j * LN:(j + 1) * LN]
            flat[pl.ds(VEC_ROW + 52, 12), :] = jnp.zeros((12, LN), F32)
            end = ROWS
        while sent < 16 and window_start(2 * sent + 1) + WIN <= end:
            s0_copy(sent, 0).start()
            sent += 1
            if sent > 1:
                s0_add(sent - 2, 0)
    s0_add(15, 0)
    for i in range(16):
        s0_copy(i, 1).start()

    recv = (r1, r2, r3, r4)
    both = pl.ds(0, 2)

    def rs_copy(k, t):
        o, (row, n), _ = COLORS[k]
        idx = [both] * 4
        for d in o[:t]:
            idx[d] = bits[d]
        idx[o[t]] = 1 - bits[o[t]]
        dst = recv[t].at[(both,) * (3 - t) + (pl.ds(row, n),)]
        return pltpu.make_async_remote_copy(acc.at[tuple(idx) + (pl.ds(row, n),)], dst, rs_s.at[k, t], rs_r.at[k, t],
                                            device_id=partner[o[t]], device_id_type=MESH)

    def rs_add(k, t):
        o, (row, n), _ = COLORS[k]
        idx = [None] * 4
        for d in o[:t + 1]:
            idx[d] = bits[d]
        rest = [d for d in range(4) if d not in o[:t + 1]]
        for combo in range(2 ** len(rest)):
            sub = tuple((combo >> (len(rest) - 1 - j)) & 1 for j in range(len(rest)))
            for j, d in enumerate(rest):
                idx[d] = sub[j]
            acc[tuple(idx) + (pl.ds(row, n),)] += recv[t][sub + (pl.ds(row, n),)]

    rs = {}

    def rs_start(k, t):
        rs[k, t] = rs_copy(k, t)
        rs[k, t].start()

    for k in range(6):
        rs_start(k, 0)
    for i in range(16):
        s0_add(i, 1)
    for k in range(6, NC):
        rs_start(k, 0)
    for t in range(4):
        for k in range(NC):
            rs[k, t].wait_recv()
            rs_add(k, t)
            if t < 3:
                rs_start(k, t + 1)

    for cp in mvw:
        cp.wait()
    q = 2 * x + c
    for case in range(4):
        @pl.when(q == case)
        def _():
            gs[...] = acc[bits + (pl.ds(2 * case, SHARD),)]

    def rows(sl):
        m_new, v_new, w_new = adam_update(gs[sl, :] / 32.0, ms[sl, :], vs[sl, :], ws[sl, :])
        mo[sl, :] = m_new
        vo[sl, :] = v_new
        wn[sl, :] = w_new
        wg[(c,) + bits + (sl,)] = w_new.astype(BF16)

    def block(i, carry):
        rows(pl.ds(pl.multiple_of(i * 16, 16), 16))
        return carry

    lax.fori_loop(0, 52, block, 0, unroll=4)
    wg[(c,) + bits + (pl.ds(832, 16),)] = jnp.zeros((16, LN), BF16)
    rows(pl.ds(832, 2))
    outs = []

    def put(pairs):
        for a, b in pairs:
            cp = pltpu.make_async_copy(a, b, out_sem.at[len(outs)])
            cp.start()
            outs.append(cp)

    def ag_idx(k, t, kept):
        o = COLORS[k][0]
        idx = [both] * 4
        for d in o[:t]:
            idx[d] = bits[d]
        if t < 4:
            idx[o[t]] = bits[o[t]] if kept else 1 - bits[o[t]]
        return (c,) + tuple(idx) + (pl.ds(*COLORS[k][2]),)

    def ag_copy(k, t):
        ref = wg.at[ag_idx(k, t, True)]
        return pltpu.make_async_remote_copy(ref, ref, ag_s.at[k, t], ag_r.at[k, t],
                                            device_id=partner[COLORS[k][0][t]], device_id_type=MESH)

    def pc_copy(k, t):
        ref = wg.at[ag_idx(k, t, False)]
        return pltpu.make_async_remote_copy(ref, ref, pc_s.at[k, t], pc_r.at[k, t],
                                            device_id=peer, device_id_type=MESH)

    ag, pc = {}, {}

    def ag_start(k, t):
        ag[k, t] = ag_copy(k, t)
        ag[k, t].start()

    def pc_start(k, t):
        pc[k, t] = pc_copy(k, t)
        pc[k, t].start()

    for k in range(NC):
        ag_start(k, 3)
    for k in range(NC):
        pc_start(k, 4)
    put(((mo, m_out), (vo, v_out), (wn, w_out)))
    for t in BACK:
        for k in range(NC):
            ag[k, t].wait_recv()
            if t > 0:
                ag_start(k, t - 1)
            pc_start(k, t)
    for cp in [rs[key] for key in rs]:
        cp.wait_send()
    for g in range(2):
        for i in range(16):
            s0_copy(i, g).wait_send()
    for t in BACK:
        for k in range(NC):
            pc[k, t].wait_recv()
    for k in range(NC):
        pc[k, 4].wait_recv()

    spread(wg, flat, range(32))
    for i, (ref, out) in enumerate(((we, we_out), (wi, wi_out), (wo, wo_out), (wa, wa_out))):
        to_native(flat, ref, (0, 2, 3, 1)[i], 1 if ref is wi else 4)
        put(((ref, out),))
    for j in range(4):
        wvd[:, j * LN:(j + 1) * LN] = flat[pl.ds(VEC_ROW + j, 9, stride=4), :].astype(BF16)
    for j in range(16):
        wvf[:, j * LN:(j + 1) * LN] = flat[pl.ds(VEC_ROW + 36 + j, 1), :].astype(BF16)
    put(((wvd, wvd_out), (wvf, wvf_out)))
    for cp in list(ag.values()) + list(pc.values()):
        cp.wait_send()
    for cp in outs:
        cp.wait()


def comm(*args):
    hbm = pl.BlockSpec(memory_space=pl.ANY)
    shard = jax.ShapeDtypeStruct((SHARD, LN), F32)
    dma = pltpu.SemaphoreType.DMA
    weights = ((VOCAB, D), (FF, D), (D, FF), (FF, D), (9, D), (1, FF))
    return pl.pallas_call(
        comm_kernel,
        out_shape=(shard,) * 3 + tuple(jax.ShapeDtypeStruct(s, BF16) for s in weights),
        in_specs=[hbm] * 9,
        out_specs=(hbm,) * 9,
        scratch_shapes=[
            pltpu.VMEM((RING[0], CHUNK // D, D), F32), pltpu.VMEM((RING[1], CHUNK // FF, FF), F32),
            pltpu.VMEM((9, D), F32), pltpu.VMEM((1, FF), F32),
            pltpu.VMEM((ROWS, LN), F32)]
        + [pltpu.VMEM((2,) * n + (WIN, LN), F32) for n in (4,) + BACK]
        + [pltpu.VMEM((SHARD, LN), F32)] * 7
        + [pltpu.VMEM((2,) * 5 + (WROWS, LN), BF16)]
        + [pltpu.VMEM(s, BF16) for s in weights]
        + [dma((sum(RING) + 2,)), dma((3,)), dma((2, 16)), dma((2, 16))]
        + [dma((NC, 4))] * 4 + [dma((NC, 5))] * 2 + [dma((9,))],
        compiler_params=pltpu.CompilerParams(collective_id=0, has_side_effects=True, vmem_limit_bytes=66_000_000),
        name="comm",
    )(*args)


TM = 1024


def ffn_kernel(tok, act, we, wa, wi, wo, wvd, wvf, m_in, v_in, w_in,
               out, we_out, wa_out, wi_out, wo_out, wvd_out, wvf_out, m_out, v_out, w_out):
    i = pl.program_id(0)

    @pl.when(i == 0)
    def _():
        for a, b in ((wvd, wvd_out), (wvf, wvf_out), (m_in, m_out), (v_in, v_out), (w_in, w_out)):
            b[...] = a[...]

    wa_out[...] = wa[...]
    for a, b in ((we, we_out), (wi, wi_out), (wo, wo_out)):
        n = b.shape[0]
        b[...] = a[pl.ds(pl.multiple_of(i * n, n), n), :]
    lane = lax.broadcasted_iota(jnp.int32, (TM, LN), 1)
    col = jnp.transpose(jnp.broadcast_to(tok[0], (LN, TM)), (1, 0))
    hot = jnp.concatenate([(col == lane + LN * j).astype(F32).astype(BF16) for j in range(VOCAB // LN)], axis=1)
    rows = jnp.dot(hot, we[...], preferred_element_type=F32)
    hidden = (rows * math.sqrt(D) + act[...].astype(F32)).astype(BF16)
    step = 512
    parts = []
    pre = jnp.dot(hidden, wi[:, 0:step], preferred_element_type=F32)
    for f in range(0, FF, step):
        nxt = None
        if f + step < FF:
            nxt = jnp.dot(hidden, wi[:, f + step:f + 2 * step], preferred_element_type=F32)
        parts.append(gelu_tanh(pre + wvf[:, f:f + step].astype(F32)).astype(BF16))
        pre = nxt
    inner = jnp.concatenate(parts, axis=1)
    total = jnp.dot(inner, wo[...], preferred_element_type=F32)
    out[...] = (total + wvd[8:9, :].astype(F32)).astype(BF16)


def ffn(tok, act, *rest):
    tokens = act.shape[0]
    steps = tokens // TM
    row = lambda i: (i, 0)

    def whole(ref):
        return pl.BlockSpec(ref.shape, lambda i: (0, 0))

    def part(ref):
        return pl.BlockSpec((ref.shape[0] // steps, ref.shape[1]), row)

    we, wa, wi, wo, wvd, wvf, m, v, w = rest
    outs = (we, wa, wi, wo, wvd, wvf, m, v, w)
    return pl.pallas_call(
        ffn_kernel,
        grid=(steps,),
        out_shape=(jax.ShapeDtypeStruct(act.shape, BF16),) + tuple(jax.ShapeDtypeStruct(a.shape, a.dtype) for a in outs),
        in_specs=[pl.BlockSpec((1, 1, TM), lambda i: (i, 0, 0)), part(act), whole(we), part(wa), whole(wi), whole(wo)]
        + [whole(a) for a in (wvd, wvf, m, v, w)],
        out_specs=(part(act), part(we), part(wa), part(wi), part(wo)) + tuple(whole(a) for a in (wvd, wvf, m, v, w)),
        compiler_params=pltpu.CompilerParams(vmem_limit_bytes=66_000_000),
        name="ffn",
    )(tok.reshape(steps, 1, TM), act, *rest)


def solution(mesh):
    def device_step(g_emb, g_attn, g_in, g_out, g_vecd, g_vecf, opt_m, opt_v, master, tok_ids, act_in):
        m1, v1, w1, *weights = comm(
            g_emb.reshape(VOCAB, D), g_attn.reshape(FF, D), g_in.reshape(D, FF), g_out.reshape(FF, D),
            g_vecd.reshape(9, D), g_vecf.reshape(1, FF),
            opt_m.reshape(SHARD, LN), opt_v.reshape(SHARD, LN), master.reshape(SHARD, LN))
        y_out, we, wa, wi, wo, wvd, wvf, m_new, v_new, w_new = ffn(tok_ids, act_in, *weights, m1, v1, w1)
        return (m_new.reshape(-1), v_new.reshape(-1), w_new.reshape(-1), we, wa.reshape(1, 4, D, D),
                wi.reshape(1, D, FF), wo.reshape(1, FF, D), wvd.reshape(1, 9, D), wvf, y_out)

    grad_specs = tuple(P(AXES, *([None] * (grad_rank - 1))) for grad_rank in GRAD_RANKS)
    in_specs = grad_specs + (P(AXES), P(AXES), P(AXES), P(AXES), P(AXES, None))
    out_specs = (P(AXES), P(AXES), P(AXES), P(), P(), P(), P(), P(), P(), P(AXES, None))
    return jax.shard_map(device_step, mesh=mesh, in_specs=in_specs, out_specs=out_specs, check_vma=False)
```

time: 743 us -> 211 us (0.28)
  waiting for transfers between devices: 346 us -> 0 us
  Pallas kernels: 0 us -> 209 us
  other arithmetic: 145 us -> 0 us
  local copies, waits for them, and re-layouts: 120 us -> 1.34 us
  matrix products: 117 us -> 0 us
  between operations: 14.2 us -> 0.65 us
    unnamed x3 -> x0, waiting for transfers between devices: 246 us -> none
    pallas_call x0 -> x2, Pallas kernels: none -> 209 us  [the longest x1 114 us: comm(): pl.pallas_call(comm_kernel, out_shape=(shard,) * 3 + tuple((jax.ShapeDtyp...]
    all_gather x1 -> x0, other arithmetic: 141 us -> none  [device_step(): lax.all_gather(w_new.astype(jnp.bfloat16), AXES, axis=0, tiled=True)]
    dot_general x2 -> x0, matrix products: 117 us -> none  [the longest x1 73 us: ffn_block(): jnp.dot(hidden, w_in, preferred_element_type=jnp.float32)]
    all_gather x1 -> x0, waiting for transfers between devices: 100 us -> none  [device_step(): lax.all_gather(w_new.astype(jnp.bfloat16), AXES, axis=0, tiled=True)]
    gather x1 -> x0, local copies, waits for them, and re-layouts: 66.4 us -> none  [ffn_block(): emb_rows = jnp.take(wb_emb, tok_ids, axis=0).astype(jnp.float32)]
    unnamed x31 -> x1, local copies, waits for them, and re-layouts: 24 us -> 1.34 us
    slice x8 -> x0, local copies, waits for them, and re-layouts: 12.3 us -> none  [split_flat(): pieces.append(flat_vals[offset:offset + elem_count].reshape(tensor_shape))]
  transfers between devices with their start and end apart: 2 -> 0, of which waited for: 2 -> 0; matrix products, arithmetic and copies ran while one was open for 0% -> 0% of each run, Pallas kernels for 0% -> 0%
where the time goes in v3:
time: 211 us
  Pallas kernels  209 us (99%)
    pallas_call x1, Pallas kernels, comm(): pl.pallas_call(comm_kernel, out_shape=(shard,) * 3 + tuple((jax.ShapeDtyp...  114 us
    pallas_call x1, Pallas kernels, ffn(): pl.pallas_call(ffn_kernel, grid=(steps,), out_shape=(jax.ShapeDtypeStruct...  94.6 us

profile of v3, /device:TPU:1, one launch (start us, length us, event | category | flops | bytes accessed | tf_op | source)
XLA Modules:
  0.0 210.8 jit_solution(4590318562404202393)
XLA Ops:
  0.6 1.3 copy.23
  2.0 114.2 %comm.1 = (f32[834,128]{1,0:T(8,128)}, f32[834,128]{1,0:T(8,128)}, f32[834,128]{1,0:T(8,128)}, bf16[512,512]{1,0:T(8,128)(2,1)}, bf16[2048,512]{1,0:T(8,128)(2,1...) custom-call(f32[512,512]{1,0:T(8,128)} %bitcast.22, ...), custom_call_target="tpu_custom_call" | custom-call | tf_op jit(solution)/shard_map/comm/pallas_call | solution.py:331
  116.2 94.6 %ffn.1 = (bf16[16384,512]{1,0:T(8,128)(2,1)}, bf16[512,512]{1,0:T(8,128)(2,1)}, bf16[2048,512]{1,0:T(8,128)(2,1)}, bf16[512,2048]{1,0:T(8,128)(2,1)}, bf16[2048,...) custom-call(s32[16,1,1024]{2,1,0:T(1,128)} %bitcast.27, ...), custom_call_target="tpu_custom_call" | custom-call | tf_op jit(solution)/shard_map/ffn/pallas_call | solution.py:399

commit v4 on v3

--- a/solution.py
+++ b/solution.py
@@ -29,10 +29,11 @@
 BACK = (3, 2, 1, 0)
 ORDERS = ((X, Y, ZA, ZB), (X, Y, ZB, ZA), (Y, X, ZA, ZB), (Y, X, ZB, ZA), (ZA, ZB, X, Y), (ZB, ZA, Y, X))
 RS_ROWS = (72, 64, 72, 64, 72, 72, 72, 72, 72, 72, 64, 72)
-AG_ROWS = (80, 64, 80, 64, 64, 64, 80, 64, 80, 64, 64, 80)
+AG_ROWS = (64, 64, 64, 64, 64, 80, 80, 64, 80, 80, 64, 80)
 NC = len(RS_ROWS)
 COLORS = tuple((ORDERS[k % len(ORDERS)], (sum(RS_ROWS[:k]), RS_ROWS[k]), (sum(AG_ROWS[:k]), AG_ROWS[k]))
                for k in range(NC))
+EARLY_ROWS = sum(AG_ROWS[:6])
 GROUPS = ((0, sum(RS_ROWS[:6])), (sum(RS_ROWS[:6]), sum(RS_ROWS[6:])))
 CHUNK, CHUNK_ROWS = 131072, 1024
 RING = 6, 4
@@ -61,10 +62,10 @@
     return half + half * jnp.tanh(v * (c + (c * 0.044715) * (v * v)))
 
 
-def spread(wg, flat, shards):
-    for s in shards:
+def spread(wg, flat, row, n):
+    for s in range(32):
         idx = (s % 2,) + slot(s // 2)
-        flat[pl.ds(s * SHARD, SHARD), :] = wg[idx + (pl.ds(0, SHARD),)].astype(F32)
+        flat[pl.ds(s * SHARD + row, n), :] = wg[idx + (pl.ds(row, n),)].astype(F32)
 
 
 def to_native(flat, dst, tensor, unroll):
@@ -220,20 +221,18 @@
         s0_add(i, 1)
     for k in range(6, NC):
         rs_start(k, 0)
-    for t in range(4):
+    def rs_take(k, t):
+        rs[k, t].wait_recv()
+        rs_add(k, t)
+        if t < 3:
+            rs_start(k, t + 1)
+
+    for t in range(3):
         for k in range(NC):
-            rs[k, t].wait_recv()
-            rs_add(k, t)
-            if t < 3:
-                rs_start(k, t + 1)
+            rs_take(k, t)
 
     for cp in mvw:
         cp.wait()
-    q = 2 * x + c
-    for case in range(4):
-        @pl.when(q == case)
-        def _():
-            gs[...] = acc[bits + (pl.ds(2 * case, SHARD),)]
 
     def rows(sl):
         m_new, v_new, w_new = adam_update(gs[sl, :] / 32.0, ms[sl, :], vs[sl, :], ws[sl, :])
@@ -242,13 +241,21 @@
         wn[sl, :] = w_new
         wg[(c,) + bits + (sl,)] = w_new.astype(BF16)
 
-    def block(i, carry):
-        rows(pl.ds(pl.multiple_of(i * 16, 16), 16))
-        return carry
-
-    lax.fori_loop(0, 52, block, 0, unroll=4)
-    wg[(c,) + bits + (pl.ds(832, 16),)] = jnp.zeros((16, LN), BF16)
-    rows(pl.ds(832, 2))
+    def adam(row, n):
+        for case in range(4):
+            @pl.when(2 * x + c == case)
+            def _():
+                gs[pl.ds(row, n), :] = acc[bits + (pl.ds(row + 2 * case, n),)]
+
+        def block(i, carry):
+            rows(pl.ds(pl.multiple_of(row + i * 16, 16), 16))
+            return carry
+
+        lax.fori_loop(0, n // 16, block, 0, unroll=5 if row == 0 else 3)
+        if n % 16:
+            wg[(c,) + bits + (pl.ds(832, 16),)] = jnp.zeros((16, LN), BF16)
+            rows(pl.ds(832, 2))
+
     outs = []
 
     def put(pairs):
@@ -286,29 +293,40 @@
         pc[k, t] = pc_copy(k, t)
         pc[k, t].start()
 
-    for k in range(NC):
+    for k in range(6):
+        rs_take(k, 3)
+    adam(0, EARLY_ROWS)
+    for k in range(6):
+        ag_start(k, 3)
+    for k in range(6, NC):
+        rs_take(k, 3)
+    adam(EARLY_ROWS, SHARD - EARLY_ROWS)
+    for k in range(6, NC):
         ag_start(k, 3)
     for k in range(NC):
         pc_start(k, 4)
     put(((mo, m_out), (vo, v_out), (wn, w_out)))
-    for t in BACK:
+    for t in BACK[:3]:
         for k in range(NC):
             ag[k, t].wait_recv()
-            if t > 0:
-                ag_start(k, t - 1)
+            ag_start(k, t - 1)
             pc_start(k, t)
     for cp in [rs[key] for key in rs]:
         cp.wait_send()
     for g in range(2):
         for i in range(16):
             s0_copy(i, g).wait_send()
-    for t in BACK:
-        for k in range(NC):
-            pc[k, t].wait_recv()
-    for k in range(NC):
-        pc[k, 4].wait_recv()
-
-    spread(wg, flat, range(32))
+    for part in (range(6), range(6, NC)):
+        for k in part:
+            ag[k, 0].wait_recv()
+            pc_start(k, 0)
+        for k in part:
+            for t in range(5):
+                pc[k, t].wait_recv()
+        if part[0] == 0:
+            spread(wg, flat, 0, EARLY_ROWS)
+    spread(wg, flat, EARLY_ROWS, SHARD - EARLY_ROWS)
+
     for i, (ref, out) in enumerate(((we, we_out), (wi, wi_out), (wo, wo_out), (wa, wa_out))):
         to_native(flat, ref, (0, 2, 3, 1)[i], 1 if ref is wi else 4)
         put(((ref, out),))

time: 211 us -> 210 us (level)
  no operation moved by 1% of the time
where the time goes in v4:
time: 210 us; the launch traced here: 209 us
  Pallas kernels  207 us (99%)
    pallas_call x1, Pallas kernels, comm(): pl.pallas_call(comm_kernel, out_shape=(shard,) * 3 + tuple((jax.ShapeDtyp...  113 us
    pallas_call x1, Pallas kernels, ffn(): pl.pallas_call(ffn_kernel, grid=(steps,), out_shape=(jax.ShapeDtypeStruct...  94.6 us

profile of v4, /device:TPU:1, one launch (start us, length us, event | category | flops | bytes accessed | tf_op | source)
XLA Modules:
  0.0 209.3 jit_solution(2382130171169946059)
XLA Ops:
  0.6 1.3 copy.23
  2.0 112.7 %comm.1 = (f32[834,128]{1,0:T(8,128)}, f32[834,128]{1,0:T(8,128)}, f32[834,128]{1,0:T(8,128)}, bf16[512,512]{1,0:T(8,128)(2,1)}, bf16[2048,512]{1,0:T(8,128)(2,1...) custom-call(f32[512,512]{1,0:T(8,128)} %bitcast.22, ...), custom_call_target="tpu_custom_call" | custom-call | tf_op jit(solution)/shard_map/comm/pallas_call | solution.py:349
  114.7 94.6 %ffn.1 = (bf16[16384,512]{1,0:T(8,128)(2,1)}, bf16[512,512]{1,0:T(8,128)(2,1)}, bf16[2048,512]{1,0:T(8,128)(2,1)}, bf16[512,2048]{1,0:T(8,128)(2,1)}, bf16[2048,...) custom-call(s32[16,1,1024]{2,1,0:T(1,128)} %bitcast.27, ...), custom_call_target="tpu_custom_call" | custom-call | tf_op jit(solution)/shard_map/ffn/pallas_call | solution.py:417

commit v5 on v4

--- a/solution.py
+++ b/solution.py
@@ -170,7 +170,7 @@
             for cp in vec:
                 cp.wait()
             for j in range(4):
-                flat[pl.ds(VEC_ROW + j, 9, stride=4), :] = svd[:, j * LN:(j + 1) * LN]
+                flat[pl.ds(VEC_ROW + j, 9, stride=4), :] = svd[:, 0, j * LN:(j + 1) * LN]
             for j in range(16):
                 flat[pl.ds(VEC_ROW + 36 + j, 1), :] = svf[:, j * LN:(j + 1) * LN]
             flat[pl.ds(VEC_ROW + 52, 12), :] = jnp.zeros((12, LN), F32)
@@ -353,7 +353,7 @@
         out_specs=(hbm,) * 9,
         scratch_shapes=[
             pltpu.VMEM((RING[0], CHUNK // D, D), F32), pltpu.VMEM((RING[1], CHUNK // FF, FF), F32),
-            pltpu.VMEM((9, D), F32), pltpu.VMEM((1, FF), F32),
+            pltpu.VMEM((9, 1, D), F32), pltpu.VMEM((1, FF), F32),
             pltpu.VMEM((ROWS, LN), F32)]
         + [pltpu.VMEM((2,) * n + (WIN, LN), F32) for n in (4,) + BACK]
         + [pltpu.VMEM((SHARD, LN), F32)] * 7
@@ -430,7 +430,7 @@
     def device_step(g_emb, g_attn, g_in, g_out, g_vecd, g_vecf, opt_m, opt_v, master, tok_ids, act_in):
         m1, v1, w1, *weights = comm(
             g_emb.reshape(VOCAB, D), g_attn.reshape(FF, D), g_in.reshape(D, FF), g_out.reshape(FF, D),
-            g_vecd.reshape(9, D), g_vecf.reshape(1, FF),
+            g_vecd.reshape(9, 1, D), g_vecf.reshape(1, FF),
             opt_m.reshape(SHARD, LN), opt_v.reshape(SHARD, LN), master.reshape(SHARD, LN))
         y_out, we, wa, wi, wo, wvd, wvf, m_new, v_new, w_new = ffn(tok_ids, act_in, *weights, m1, v1, w1)
         return (m_new.reshape(-1), v_new.reshape(-1), w_new.reshape(-1), we, wa.reshape(1, 4, D, D),

time: 210 us -> 208 us (level)
  no operation moved by 1% of the time
where the time goes in v5:
time: 208 us
  Pallas kernels  207 us (100%)
    pallas_call x1, Pallas kernels, comm(): pl.pallas_call(comm_kernel, out_shape=(shard,) * 3 + tuple((jax.ShapeDtyp...  113 us
    pallas_call x1, Pallas kernels, ffn(): pl.pallas_call(ffn_kernel, grid=(steps,), out_shape=(jax.ShapeDtypeStruct...  94.6 us

profile of v5, /device:TPU:1, one launch (start us, length us, event | category | flops | bytes accessed | tf_op | source)
XLA Modules:
  0.0 208.0 jit_solution(16273666669907738940)
XLA Ops:
  0.6 112.7 %comm.1 = (f32[834,128]{1,0:T(8,128)}, f32[834,128]{1,0:T(8,128)}, f32[834,128]{1,0:T(8,128)}, bf16[512,512]{1,0:T(8,128)(2,1)}, bf16[2048,512]{1,0:T(8,128)(2,1...) custom-call(f32[512,512]{1,0:T(8,128)} %bitcast.20, ...), custom_call_target="tpu_custom_call" | custom-call | tf_op jit(solution)/shard_map/comm/pallas_call | solution.py:349
  113.4 94.6 %ffn.1 = (bf16[16384,512]{1,0:T(8,128)(2,1)}, bf16[512,512]{1,0:T(8,128)(2,1)}, bf16[2048,512]{1,0:T(8,128)(2,1)}, bf16[512,2048]{1,0:T(8,128)(2,1)}, bf16[2048,...) custom-call(s32[16,1,1024]{2,1,0:T(1,128)} %bitcast.24, ...), custom_call_target="tpu_custom_call" | custom-call | tf_op jit(solution)/shard_map/ffn/pallas_call | solution.py:417
